TPU v7x, 32 devices: a whole 2x2x4 slice. The times are simulated.
32 devices in a mesh: dp: 8 (over z, x), tensor: 4 (over y, core).
Axes of the slice: x: 2, y: 2, z: 4, core: 2. Of those that a mesh axis runs over, the one named last changes fastest.
Arguments:
- logits: bfloat16 [16, 128, 19456], P('dp', None, 'tensor'), may hold values from -110 to 290
- token_ids: int32 [16, 128], P('dp'), may hold values from 0 to 19455
- response_mask: int32 [16, 128], P('dp'), may hold values 0 or 1
- lengths: int32 [16], P('dp'), may hold values from 16 to 128
- prompt_of: int32 [16], P('dp'), may hold values from 0 to 1, as said below
- old_logprob: float32 [16, 128], P('dp'), may hold values from -14 to -10
- ref_logprob: bfloat16 [16, 128], P(None, 'dp'), may hold values from -14 to -10
- advantages: float32 [16, 128], P('dp'), may hold values from -8 to 8
- returns: float32 [16, 128], P('dp'), may hold values from -6 to 6
- critic_hidden: bfloat16 [16, 128, 5120], P(None, 'dp', 'tensor'), may hold values from -6 to 6
- value_weight: bfloat16 [5120], P('tensor'), may hold values from -0.078125 to 0.078125
Outputs:
- token_loss: float32 [16, 128], P('dp')
- critic_grad: bfloat16 [16, 128, 5120], P(None, 'dp', 'tensor')
Inputs may be any that keep to these rules, and one draw needn't show every extreme that they name: `prompt_of`: each of the 2 prompts is named by exactly 8 sequences.
All inputs are finite; a program needn't handle non-finite values. No bound on the sum of `response_mask` on one device may be relied on, other than what follows from the above.
Results may differ from a plain program's by a relative error of at most 0.001.
Values may be sent and summed in bfloat16 or wider, within the bound.
A program may use at most 64 MiB of HBM per device.

v0:
```python
import jax
import jax.numpy as jnp
from jax import lax
from jax.sharding import PartitionSpec as P

RESPONSES = 8


def per_device(
    logits,
    token_ids,
    response_mask,
    lengths,
    prompt_of,
    old_logprob,
    ref_logprob,
    advantages,
    returns,
    critic_hidden,
    value_weight,
):
    highest = lax.Precision.HIGHEST
    seq_rows, seq_len, vocab_width = logits.shape
    all_seqs, tile_len, feat_count = critic_hidden.shape
    dp_size = lax.axis_size("dp")
    head_weight = value_weight.astype(jnp.float32)
    tile_rows = critic_hidden.reshape(all_seqs * tile_len, feat_count)
    local_part = jnp.dot(tile_rows, value_weight, preferred_element_type=jnp.float32).reshape(
        all_seqs, tile_len
    )
    partial_value, ref_rows = (
        lax.all_to_all(local_part, "dp", split_axis=0, concat_axis=1, tiled=True),
        lax.all_to_all(
            ref_logprob.astype(jnp.float32), "dp", split_axis=0, concat_axis=1, tiled=True
        ),
    )
    position = lax.broadcasted_iota(jnp.int32, (seq_rows, seq_len), 1)
    live_mask = (response_mask * (position < lengths[:, None]).astype(jnp.int32)).astype(
        jnp.float32
    )
    prompt_count = seq_rows * dp_size // RESPONSES
    prompt_hot = (
        prompt_of[:, None] == lax.broadcasted_iota(jnp.int32, (seq_rows, prompt_count), 1)
    ).astype(jnp.float32)
    seq_tokens = jnp.sum(live_mask, axis=1)
    seq_total = jnp.sum(live_mask * advantages, axis=1)
    seq_square = jnp.sum(live_mask * advantages * advantages, axis=1)
    moments = jnp.dot(jnp.stack([seq_tokens, seq_total, seq_square]), prompt_hot, precision=highest)
    count_all, total_all, square_all = lax.psum((moments[0], moments[1], moments[2]), "dp")
    count_floor = jnp.maximum(count_all, 1.0)
    prompt_mean = total_all / count_floor
    prompt_var = (square_all - prompt_mean * total_all) / count_floor
    row_mean = jnp.dot(prompt_hot, prompt_mean, precision=highest)
    row_scale = lax.rsqrt(jnp.dot(prompt_hot, prompt_var, precision=highest) + 1.0)
    whitened = (advantages - row_mean[:, None]) * row_scale[:, None]
    local_top = jnp.max(logits, axis=2).astype(jnp.float32)
    local_sum = jnp.sum(jnp.exp(logits.astype(jnp.float32) - local_top[:, :, None]), axis=2)
    vocab_start = lax.axis_index("tensor") * vocab_width
    shifted = token_ids - vocab_start
    in_shard = (shifted >= 0) & (shifted < vocab_width)
    clipped_ids = jnp.clip(shifted, 0, vocab_width - 1)
    picked = jnp.take_along_axis(logits, clipped_ids[:, :, None], axis=2)[:, :, 0].astype(
        jnp.float32
    )
    target_part = jnp.where(in_shard, picked, 0.0)
    row_max = lax.pmax(local_top, "tensor")
    rescaled = local_sum * jnp.exp(local_top - row_max)
    total_sum, target_logit, value_pred = lax.psum((rescaled, target_part, partial_value), "tensor")
    logprob = target_logit - (row_max + jnp.log(total_sum))
    prob_ratio = jnp.exp(jnp.clip(logprob - old_logprob, -20.0, 20.0))
    surrogate = jnp.maximum(-whitened * prob_ratio, -whitened * jnp.clip(prob_ratio, 0.8, 1.2))
    surrogate = jnp.where(whitened < 0.0, jnp.minimum(surrogate, -3.0 * whitened), surrogate)
    ref_drift = jnp.clip(ref_rows - logprob, -20.0, 20.0)
    penalty = jnp.clip(jnp.exp(ref_drift) - ref_drift - 1.0, -10.0, 10.0)
    value_error = value_pred - returns
    token_loss = live_mask * (surrogate + 0.1 * penalty + 0.25 * value_error * value_error)
    grad_coeff = 32.0 * live_mask * value_error
    returned = lax.all_to_all(grad_coeff, "dp", split_axis=1, concat_axis=0, tiled=True)
    critic_grad = (returned[:, :, None] * head_weight[None, None, :]).astype(jnp.bfloat16)
    return (token_loss, critic_grad)


def solution(mesh):
    in_specs = (
        P("dp", None, "tensor"),
        P("dp", None),
        P("dp", None),
        P("dp"),
        P("dp"),
        P("dp", None),
        P(None, "dp"),
        P("dp", None),
        P("dp", None),
        P(None, "dp", "tensor"),
        P("tensor"),
    )
    out_specs = (P("dp", None), P(None, "dp", "tensor"))
    return jax.shard_map(
        per_device, mesh=mesh, in_specs=in_specs, out_specs=out_specs, check_vma=False
    )
```

profile of v0, /device:TPU:0, one launch (start us, length us, event | category | flops | bytes accessed | tf_op | source)
XLA Modules:
  0.0 71.6 jit_solution(9083070051270361440)
XLA Ops:
  0.6 0.0 copy-start
  0.6 0.0 copy-start.1
  0.7 1.4 %convert.1 = f32[8,2,16]{2,1,0:T(2,128)} convert(bf16[8,2,16]{2,1,0:T(2,128)(2,1)} %bitcast.45) | non-fusion elementwise | flops 256 | bytes 1536 | tf_op jit(solution)/shard_map/all_to_all | solution.py:33
  2.1 7.3 %all-to-all-start = ((f32[8,2,16]{2,1,0:T(2,128)}), f32[8,2,16]{2,1,0:T(2,128)S(1)}, u32[]{:S(2)}, u32[]{:S(2)}) async-start(f32[8,2,16]{2,1,0:T(2,128)} %convert.1), calls=%async_computation | async-start | bytes 16384 | tf_op jit(solution)/shard_map/all_to_all | solution.py:33
  9.4 0.0 copy-start.2
  9.4 0.0 copy-start.3
  9.4 2.1 %reduce_max.9 = bf16[2,128]{1,0:T(2,128)(2,1)S(1)} reduce(bf16[2,128,4864]{2,1,0:T(8,128)(2,1)} %param.11, bf16[]{:T(256)} %constant.27.clone.1), dimensions={2}, to_apply=%region_7.0 | reduce | flops 1244928 | bytes 2490882 | tf_op jit(solution)/shard_map/reduce_max | solution.py:56
  11.5 0.0 copy-start.5
  11.5 0.0 copy-start.6
  11.5 0.0 copy-start.8
  11.6 0.0 copy-start.4
  11.6 0.0 copy-start.9
  11.6 0.0 copy-start.7
  11.6 6.6 %pmax.7 = f32[2,128]{1,0:T(2,128)S(1)} all-reduce(bf16[2,128]{1,0:T(2,128)(2,1)S(1)} %reduce_max.9), channel_id=1, replica_groups=mesh['dp'=8,'tensor'=4] {'tensor'}, use_global_device_ids=true, to_apply=%region_8.9 | all-reduce | flops 256 | bytes 1536 | tf_op jit(solution)/shard_map/pmax | solution.py:66
  18.2 0.0 copy-done.1
  18.2 1.0 %exponential_reduce_fusion = f32[2,128]{1,0:T(2,128)S(1)} fusion(bf16[2,128,4864]{2,1,0:T(8,128)(2,1)S(1)} %copy-done.1, f32[2,128]{1,0:T(2,128)S(1)} %convert_element_type.27), kind=kLoop, calls=%fused_computation.1 | loop fusion | flops 3735296 | bytes 2492416 | tf_op jit(solution)/shard_map/reduce_sum | solution.py:57
  19.2 0.0 copy-done.2
  19.2 0.0 copy-done.3
  19.3 0.0 copy-done
  19.3 1.5 %fusion.2 = f32[1,8,2,16]{3,0,2,1:T(1,128)} fusion(bf16[8,2,16,1280]{3,2,1,0:T(8,128)(2,1)S(1)} %bitcast.41, bf16[1280,1,1,1]{0,1,2,3:T(2,128)(2,1)S(1)} %reshape.68), kind=kOutput, calls=%fused_computation.7 | convolution fusion | flops 655360 | bytes 658944 | tf_op jit(solution)/shard_map/dot_general | solution.py:28
  20.8 2.8 %gather_fusion = bf16[256]{0:T(256)(128)(2,1)S(1)} fusion(bf16[2,128,4864]{2,1,0:T(8,128)(2,1)S(1)} %copy-done.1, s32[256]{0:T(256)S(1)} %fusion.18), kind=kCustom, calls=%fused_computation | custom fusion | bytes 4096 | tf_op jit(solution)/shard_map/jit(take_along_axis)/gather | solution.py:62
  23.6 0.0 all-to-all-done
  23.6 5.4 %all-to-all-start.1 = ((f32[8,2,16]{2,1,0:T(2,128)}), f32[8,2,16]{2,1,0:T(2,128)S(1)}, u32[]{:S(2)}, u32[]{:S(2)}) async-start(f32[8,2,16]{2,1,0:T(2,128)} %bitcast.16), calls=%async_computation.1 | async-start | bytes 16384 | tf_op jit(solution)/shard_map/all_to_all | solution.py:32
  29.1 0.1 all_to_all.44
  29.1 6.4 %all-to-all-done.1 = f32[8,2,16]{2,1,0:T(2,128)S(1)} async-done(((f32[8,2,16]{2,1,0:T(2,128)}), f32[8,2,16]{2,1,0:T(2,128)S(1)}, u32[]{:S(2)}, u32[]{:S(2)}) %all-to-all-start.1) | async-done | bytes 1056 | tf_op jit(solution)/shard_map/all_to_all | solution.py:32
  35.5 0.1 all_to_all.47
  35.6 5.6 %all-reduce.1 = (f32[2,128]{1,0:T(2,128)S(1)}, f32[2,128]{1,0:T(2,128)S(1)}, f32[2,128]{1,0:T(2,128)S(1)}) all-reduce(f32[2,128]{1,0:T(2,128)S(1)} %and_select_fusion.1, f32[2,128]{1,0:T(2,128)S(1)} %exponential_multiply_fusion, f32[2,128]{1,0:T(2,128)S(1)} %all_to_all.47), channel_id=1, replica_groups=mesh['dp'=8,'tensor'=4] {'tensor'}, use_global_device_ids=true, to_apply=%region_6.0 | all-reduce | flops 768 | bytes 6144 | tf_op jit(solution)/shard_map/psum | solution.py:68
  41.3 0.0 copy-done.5
  41.3 0.0 copy-done.6
  41.3 0.0 copy-done.8
  41.3 0.1 multiply_multiply_fusion.1
  41.4 0.0 copy-done.4
  41.4 0.1 multiply_reduce_fusion.1
  41.5 0.0 copy-done.9
  41.5 0.3 fusion.4
  41.8 0.2 slice_reduce_fusion.1
  42.0 17.7 %all-reduce = (f32[2]{0:T(128)S(1)}, f32[2]{0:T(128)S(1)}, f32[2]{0:T(128)S(1)}) all-reduce(f32[2]{0:T(128)S(1)} %get-tuple-element.5, f32[2]{0:T(128)S(1)} %get-tuple-element.6, f32[2]{0:T(128)S(1)} %get-tuple-element.4), channel_id=1, replica_groups=mesh['dp'=8,'tensor'=4] {'dp'}, use_global_device_ids=true, to_apply=%region_5.0 | all-reduce | flops 6 | bytes 48 | tf_op jit(solution)/shard_map/psum | solution.py:49
  59.7 0.2 convolution_bitcast_fusion.1
  59.9 0.2 fusion.1
  60.1 0.1 all_to_all.48
  60.2 0.6 copy.19
  60.8 3.3 %all-to-all-start.2 = ((f32[2,8,16]{2,0,1:T(2,128)}), f32[2,8,16]{2,0,1:T(2,128)S(1)}, u32[]{:S(2)}, u32[]{:S(2)}) async-start(f32[2,8,16]{2,0,1:T(2,128)} %copy.19), calls=%async_computation.2 | async-start | bytes 16384 | tf_op jit(solution)/shard_map/all_to_all | solution.py:78
  64.1 0.0 copy-done.7
  64.1 0.6 fusion.22
  64.8 5.8 %all-to-all-done.2 = f32[2,8,16]{2,0,1:T(2,128)S(1)} async-done(((f32[2,8,16]{2,0,1:T(2,128)}), f32[2,8,16]{2,0,1:T(2,128)S(1)}, u32[]{:S(2)}, u32[]{:S(2)}) %all-to-all-start.2) | async-done | bytes 1056 | tf_op jit(solution)/shard_map/all_to_all | solution.py:78
  70.6 1.0 %multiply_convert_fusion = bf16[16,16,1280]{2,1,0:T(8,128)(2,1)} fusion(f32[1280]{0:T(1024)S(1)} %convert_element_type.29, f32[16,16]{1,0:T(8,128)S(1)} %bitcast.42), kind=kLoop, calls=%fused_computation.2 | loop fusion | flops 655360 | bytes 661504 | tf_op jit(solution)/shard_map/convert_element_type | solution.py:79
  (13 shorter events, 0.1 us)
Async XLA Ops:
  0.6 18.6 %copy-start = (bf16[16,16,1280]{2,1,0:T(8,128)(2,1)S(1)}, bf16[16,16,1280]{2,1,0:T(8,128)(2,1)}, u32[]{:S(2)}) copy-start(bf16[16,16,1280]{2,1,0:T(8,128)(2,1)} %param.20) | copy-start | bytes 1966084
  0.6 17.6 %copy-start.1 = (bf16[2,128,4864]{2,1,0:T(8,128)(2,1)S(1)}, bf16[2,128,4864]{2,1,0:T(8,128)(2,1)}, u32[]{:S(2)}) copy-start(bf16[2,128,4864]{2,1,0:T(8,128)(2,1)} %param.11) | copy-start | bytes 7471108
  2.1 21.5 %all-to-all-start = ((f32[8,2,16]{2,1,0:T(2,128)}), f32[8,2,16]{2,1,0:T(2,128)S(1)}, u32[]{:S(2)}, u32[]{:S(2)}) async-start(f32[8,2,16]{2,1,0:T(2,128)} %convert.1), calls=%async_computation | async-start | bytes 16384 | tf_op jit(solution)/shard_map/all_to_all | solution.py:33
  9.4 9.8 %copy-start.2 = (bf16[1280]{0:T(1024)(128)(2,1)S(1)}, bf16[1280]{0:T(1024)(128)(2,1)}, u32[]{:S(2)}) copy-start(bf16[1280]{0:T(1024)(128)(2,1)} %param.21) | copy-start | bytes 7684
  9.4 9.8 %copy-start.3 = (s32[2,128]{1,0:T(2,128)S(1)}, s32[2,128]{1,0:T(2,128)}, u32[]{:S(2)}) copy-start(s32[2,128]{1,0:T(2,128)} %param.12) | copy-start | bytes 3076
  11.5 29.7 %copy-start.5 = (f32[2,128]{1,0:T(2,128)S(1)}, f32[2,128]{1,0:T(2,128)}, u32[]{:S(2)}) copy-start(f32[2,128]{1,0:T(2,128)} %param.19) | copy-start | bytes 3076
  11.5 29.7 %copy-start.6 = (s32[2,128]{1,0:T(2,128)S(1)}, s32[2,128]{1,0:T(2,128)}, u32[]{:S(2)}) copy-start(s32[2,128]{1,0:T(2,128)} %param.13) | copy-start | bytes 3076
  11.5 29.7 %copy-start.8 = (s32[2]{0:T(128)S(1)}, s32[2]{0:T(128)}, u32[]{:S(2)}) copy-start(s32[2]{0:T(128)} %param.14) | copy-start | bytes 28
  11.6 29.8 %copy-start.4 = (f32[2,128]{1,0:T(2,128)S(1)}, f32[2,128]{1,0:T(2,128)}, u32[]{:S(2)}) copy-start(f32[2,128]{1,0:T(2,128)} %param.18) | copy-start | bytes 3076
  11.6 29.9 %copy-start.9 = (s32[2]{0:T(128)S(1)}, s32[2]{0:T(128)}, u32[]{:S(2)}) copy-start(s32[2]{0:T(128)} %param.15) | copy-start | bytes 28
  11.6 52.5 %copy-start.7 = (f32[2,128]{1,0:T(2,128)S(1)}, f32[2,128]{1,0:T(2,128)}, u32[]{:S(2)}) copy-start(f32[2,128]{1,0:T(2,128)} %param.16) | copy-start | bytes 3076
  23.6 12.0 %all-to-all-start.1 = ((f32[8,2,16]{2,1,0:T(2,128)}), f32[8,2,16]{2,1,0:T(2,128)S(1)}, u32[]{:S(2)}, u32[]{:S(2)}) async-start(f32[8,2,16]{2,1,0:T(2,128)} %bitcast.16), calls=%async_computation.1 | async-start | bytes 16384 | tf_op jit(solution)/shard_map/all_to_all | solution.py:32
  60.8 9.8 %all-to-all-start.2 = ((f32[2,8,16]{2,0,1:T(2,128)}), f32[2,8,16]{2,0,1:T(2,128)S(1)}, u32[]{:S(2)}, u32[]{:S(2)}) async-start(f32[2,8,16]{2,0,1:T(2,128)} %copy.19), calls=%async_computation.2 | async-start | bytes 16384 | tf_op jit(solution)/shard_map/all_to_all | solution.py:78
where the time goes:
time: 71.9 us; the launch traced here: 71.6 us
  blocking collectives  30 us (42%)
  starting transfers between devices  16 us (22%)
  waiting for transfers between devices  12.2 us (17%)
  other arithmetic  6.42 us (9%)
  local copies, waits for them, and re-layouts  3.95 us (5%)
  matrix products  2.1 us (3%)
  between operations  0.83 us (1%)
    psum x1, blocking collectives, per_device(): lax.psum((moments[0], moments[1], moments[2]), 'dp')  17.7 us
    all_to_all x1, starting transfers between devices, per_device(): lax.all_to_all(ref_logprob.astype(jnp.float32), 'dp', split_axis=0, conca...  7.28 us
    pmax x1, blocking collectives, per_device(): row_max = lax.pmax(local_top, 'tensor')  6.63 us
    all_to_all x1, waiting for transfers between devices, per_device(): lax.all_to_all(local_part, 'dp', split_axis=0, concat_axis=1, tiled=True)  6.41 us
    all_to_all x1, waiting for transfers between devices, per_device(): lax.all_to_all(grad_coeff, 'dp', split_axis=1, concat_axis=0, tiled=True)  5.8 us
    psum x1, blocking collectives, per_device(): lax.psum((rescaled, target_part, partial_value), 'tensor')  5.64 us
    all_to_all x1, starting transfers between devices, per_device(): lax.all_to_all(local_part, 'dp', split_axis=0, concat_axis=1, tiled=True)  5.43 us
    all_to_all x1, starting transfers between devices, per_device(): lax.all_to_all(grad_coeff, 'dp', split_axis=1, concat_axis=0, tiled=True)  3.33 us
  transfers between devices with their start and end apart: 3, of which 2 were waited for; matrix products, arithmetic and copies ran while one was open for 11% of the time, Pallas kernels for 0%

commit v1 on v0

v1 whole, which is shorter than its diff:
```python
import functools

import jax
import jax.numpy as jnp
from jax import lax
from jax.experimental import pallas as pl
from jax.experimental.pallas import tpu as pltpu
from jax.sharding import PartitionSpec as P

F32 = jnp.float32
BF16 = jnp.bfloat16
MESH = pl.DeviceIdType.MESH
LANES = 128
ROWS = 32


def select_dot(x, hot):
    hi = x.astype(BF16)
    rest = x - hi.astype(F32)
    mid = rest.astype(BF16)
    low = (rest - mid.astype(F32)).astype(BF16)
    n = x.shape[0]
    out = jnp.dot(jnp.concatenate([hi, mid, low], axis=0), hot, preferred_element_type=F32)
    return out[:n] + out[n : 2 * n] + out[2 * n :]


def kernel(
    dims,
    logits_hbm, ids_hbm, mask_hbm, len_hbm, prompt_hbm, old_hbm, ref_hbm, adv_hbm, ret_hbm,
    hidden_hbm, weight_hbm,
    loss_ref, coeff_ref,
    logits, ids, mask, lens, prompts, old, ref, adv, ret, hidden, weight,
    top_col, sum_col, hit_col, id_col,
    early, value_part, stats, value_sum,
    in_sem, logit_sem,
    e_send, e_recv, v_send, v_recv, s_send, s_recv, w_send, w_recv,
):
    dp, tensor, seq_rows, seq_len, vocab, all_seqs, tile = dims
    wide = seq_rows * seq_len
    me_dp = lax.axis_index("dp")
    me_t = lax.axis_index("tensor")

    smalls = [
        pltpu.make_async_copy(src, dst, in_sem.at[n])
        for n, (src, dst) in enumerate(
            [
                (hidden_hbm, hidden), (weight_hbm, weight), (ids_hbm, ids), (mask_hbm, mask),
                (len_hbm, lens), (prompt_hbm, prompts), (ref_hbm, ref), (adv_hbm, adv),
                (ret_hbm, ret), (old_hbm, old),
            ]
        )
    ]
    bigs = [
        pltpu.make_async_copy(logits_hbm.at[r], logits.at[r], logit_sem.at[r])
        for r in range(seq_rows)
    ]
    barrier = pltpu.get_barrier_semaphore()
    for d in range(1, dp):
        pl.semaphore_signal(
            barrier, inc=1, device_id=(lax.rem(me_dp + d, dp), me_t), device_id_type=MESH
        )
    for d in range(1, tensor):
        pl.semaphore_signal(
            barrier, inc=1, device_id=(me_dp, lax.rem(me_t + d, tensor)), device_id_type=MESH
        )
    for c in smalls + bigs:
        c.start()

    def over_dp(buf, send, recv):
        return [
            pltpu.make_async_remote_copy(
                src_ref=buf.at[me_dp], dst_ref=buf.at[me_dp],
                send_sem=send.at[d - 1], recv_sem=recv.at[d - 1],
                device_id=(lax.rem(me_dp + d, dp), me_t), device_id_type=MESH,
            )
            for d in range(1, dp)
        ]

    def over_tensor(buf, send, recv):
        return [
            pltpu.make_async_remote_copy(
                src_ref=buf.at[me_t], dst_ref=buf.at[me_t],
                send_sem=send.at[d - 1], recv_sem=recv.at[d - 1],
                device_id=(me_dp, lax.rem(me_t + d, tensor)), device_id_type=MESH,
            )
            for d in range(1, tensor)
        ]

    e_copies = over_dp(early, e_send, e_recv)
    v_copies = over_tensor(value_part, v_send, v_recv)
    s_copies = over_tensor(stats, s_send, s_recv)
    w_copies = over_dp(value_sum, w_send, w_recv)

    smalls[0].wait()
    smalls[1].wait()
    head = jnp.broadcast_to(weight[...], (16, weight.shape[1]))
    part = lax.dot_general(
        head, hidden[...], (((1,), (1,)), ((), ())), preferred_element_type=F32
    )
    value_part[me_t] = part[:8]

    for c in smalls[2:]:
        c.wait()

    def flat(x):
        return jnp.concatenate([x[r : r + 1] for r in range(seq_rows)], axis=1)

    lane = lax.broadcasted_iota(jnp.int32, (1, wide), 1)
    seq_of = lane // seq_len
    len_row = jnp.zeros((1, wide), jnp.int32)
    prompt_row = jnp.zeros((1, wide), jnp.int32)
    for r in range(seq_rows):
        len_row = jnp.where(seq_of == r, lens[r], len_row)
        prompt_row = jnp.where(seq_of == r, prompts[r], prompt_row)
    live = (flat(mask[...]) * (lane % seq_len < len_row).astype(jnp.int32)).astype(F32)
    adv_row = flat(adv[...])
    ret_row = flat(ret[...])
    if tile % 16 == 0:
        spread = (
            lax.broadcasted_iota(jnp.int32, (tile, wide), 0)
            == lax.broadcasted_iota(jnp.int32, (tile, wide), 1) % tile
        ).astype(F32).astype(BF16)
        ref_wide = jnp.dot(ref[...], spread, preferred_element_type=F32)
        owner = (
            lax.broadcasted_iota(jnp.int32, (all_seqs, wide), 0)
            == lax.broadcasted_iota(jnp.int32, (all_seqs, wide), 1) // tile
        )
        ref_row = jnp.sum(jnp.where(owner, ref_wide, 0.0), axis=0, keepdims=True)
    else:
        ref_row = ref[...].astype(F32)
    early[me_dp] = jnp.concatenate(
        [ret_row, live, adv_row, prompt_row.astype(F32), ref_row, jnp.zeros((3, wide), F32)],
        axis=0,
    )

    start = me_t * vocab
    lane_block = lax.broadcasted_iota(jnp.int32, (ROWS, LANES), 1)

    def column(row):
        return jnp.broadcast_to(row, (LANES, LANES)).T

    def logit_pass(r):
        bigs[r].wait()
        for h in range(seq_len // LANES):
            id_row = (ids[r : r + 1, h * LANES : (h + 1) * LANES] - start).astype(F32)
            id_col[h * LANES : (h + 1) * LANES, :] = column(id_row).astype(jnp.int32)

        def top_step(n, _):
            rows = pl.ds(pl.multiple_of(n * ROWS, ROWS), ROWS)
            top = logits[r, rows, 0:LANES]
            for c in range(1, vocab // LANES):
                top = jnp.maximum(top, logits[r, rows, c * LANES : (c + 1) * LANES])
            peak = jnp.max(top.astype(F32), axis=1, keepdims=True)
            top_col[rows, :] = jnp.broadcast_to(peak, (ROWS, LANES))
            return 0

        lax.fori_loop(0, seq_len // ROWS, top_step, 0, unroll=True)

        def sum_step(n, _):
            rows = pl.ds(pl.multiple_of(n * ROWS, ROWS), ROWS)
            peak = top_col[rows, :]
            want = id_col[rows, :]
            total = jnp.zeros((ROWS, LANES), F32)
            hit = jnp.zeros((ROWS, LANES), F32)
            for c in range(vocab // LANES):
                x = logits[r, rows, c * LANES : (c + 1) * LANES].astype(F32)
                total = total + jnp.exp(x - peak)
                hit = jnp.where(lane_block + c * LANES == want, x, hit)
            sum_col[rows, :] = total
            hit_col[rows, :] = hit
            return 0

        lax.fori_loop(0, seq_len // ROWS, sum_step, 0)
        for h in range(seq_len // LANES):
            rows = slice(h * LANES, (h + 1) * LANES)
            cols = slice(r * seq_len + h * LANES, r * seq_len + (h + 1) * LANES)
            stats[me_t, 0:1, cols] = top_col[rows, :].T[0:1]
            stats[me_t, 1:2, cols] = jnp.sum(sum_col[rows, :].T, axis=0, keepdims=True)
            stats[me_t, 2:3, cols] = jnp.sum(hit_col[rows, :].T, axis=0, keepdims=True)

    stats[me_t, 3:8, :] = jnp.zeros((5, wide), F32)
    split = (seq_rows + 1) // 2
    for r in range(split):
        logit_pass(r)
    pl.semaphore_wait(barrier, dp - 1 + tensor - 1)
    for c in v_copies + e_copies:
        c.start()
    for r in range(split, seq_rows):
        logit_pass(r)
    for c in s_copies:
        c.start()

    for c in v_copies:
        c.wait_recv()
    value = value_part[0]
    for j in range(1, tensor):
        value = value + value_part[j]
    value_sum[me_dp] = value
    for c in w_copies:
        c.start()

    for c in e_copies:
        c.wait_recv()
    rows_all = early[...].reshape(dp * 8, wide)
    k = lax.broadcasted_iota(jnp.int32, (wide, wide), 0)
    l = lax.broadcasted_iota(jnp.int32, (wide, wide), 1)
    to_tile = (k == ((l // tile) % seq_rows) * seq_len + me_dp * tile + l % tile).astype(F32)
    to_seq = (k == (me_dp * seq_rows + l // seq_len) * tile + l % tile).astype(F32)
    to_seq = to_seq.astype(BF16)
    moved = select_dot(rows_all, to_tile.astype(BF16))
    row_id = lax.broadcasted_iota(jnp.int32, (dp * 8, wide), 0)
    lane_id = lax.broadcasted_iota(jnp.int32, (dp * 8, wide), 1)
    from_seq = lane_id // (tile * seq_rows) * 8

    def fold(x, keep):
        return jnp.sum(jnp.where(keep, x, 0.0), axis=0, keepdims=True)

    ret_tile = fold(moved, row_id == from_seq)
    live_tile = fold(moved, row_id == from_seq + 1)
    coeff = 32.0 * live_tile * (value[0:1] - ret_tile)
    for h in range(wide // LANES):
        coeff_ref[h * LANES : (h + 1) * LANES, :] = column(coeff[:, h * LANES : (h + 1) * LANES])
    from_tile = (lane_id % seq_len) // tile * 8
    ref_seq = fold(select_dot(rows_all, to_seq), row_id == from_tile + 4)

    live_all = early[:, 1, :]
    adv_all = early[:, 2, :]
    prompt_all = early[:, 3, :]
    whitened = jnp.zeros((1, wide), F32)
    for r in range(seq_rows):
        same = jnp.where(prompt_all == prompts[r].astype(F32), live_all, 0.0)
        count = jnp.maximum(jnp.sum(same, keepdims=True), 1.0)
        mean = jnp.sum(same * adv_all, keepdims=True) / count
        off = adv_all - mean
        var = jnp.sum(same * off * off, keepdims=True) / count
        whitened = jnp.where(seq_of == r, (adv_row - mean) * lax.rsqrt(var + 1.0), whitened)

    for c in s_copies:
        c.wait_recv()
    row_max = stats[0, 0:1]
    for j in range(1, tensor):
        row_max = jnp.maximum(row_max, stats[j, 0:1])
    total = jnp.zeros((1, wide), F32)
    target = jnp.zeros((1, wide), F32)
    for j in range(tensor):
        total = total + stats[j, 1:2] * jnp.exp(stats[j, 0:1] - row_max)
        target = target + stats[j, 2:3]
    logprob = target - (row_max + jnp.log(total))
    prob_ratio = jnp.exp(jnp.clip(logprob - flat(old[...]), -20.0, 20.0))
    surrogate = jnp.maximum(-whitened * prob_ratio, -whitened * jnp.clip(prob_ratio, 0.8, 1.2))
    surrogate = jnp.where(whitened < 0.0, jnp.minimum(surrogate, -3.0 * whitened), surrogate)
    drift = jnp.clip(ref_seq - logprob, -20.0, 20.0)
    penalty = jnp.clip(jnp.exp(drift) - drift - 1.0, -10.0, 10.0)
    policy = surrogate + 0.1 * penalty

    for c in w_copies:
        c.wait_recv()
    value_rows = value_sum[...].reshape(dp * 8, wide)
    value_seq = fold(select_dot(value_rows, to_seq), row_id == from_tile)
    error = value_seq - ret_row
    loss = live * (policy + 0.25 * error * error)
    for r in range(seq_rows):
        loss_ref[r : r + 1, :] = loss[:, r * seq_len : (r + 1) * seq_len]
    for c in v_copies + e_copies + s_copies + w_copies:
        c.wait_send()


def per_device(
    logits, token_ids, response_mask, lengths, prompt_of, old_logprob, ref_logprob, advantages,
    returns, critic_hidden, value_weight,
):
    seq_rows, seq_len, vocab = logits.shape
    all_seqs, tile, feats = critic_hidden.shape
    dp = lax.axis_size("dp")
    tensor = lax.axis_size("tensor")
    wide = seq_rows * seq_len
    ref = ref_logprob if tile % 16 == 0 else ref_logprob.reshape(1, wide)
    args = (
        logits, token_ids, response_mask, lengths, prompt_of, old_logprob, ref, advantages,
        returns, critic_hidden.reshape(all_seqs * tile, feats), value_weight.reshape(1, feats),
    )
    scratch = [
        pltpu.SMEM(x.shape, x.dtype) if x.ndim == 1 else pltpu.VMEM(x.shape, x.dtype)
        for x in args
    ]
    scratch += [pltpu.VMEM((seq_len, LANES), t) for t in (F32, F32, F32, jnp.int32)]
    scratch += [pltpu.VMEM((n, 8, wide), F32) for n in (dp, tensor, tensor, dp)]
    dma = pltpu.SemaphoreType.DMA
    scratch += [dma((10,)), dma((seq_rows,))]
    for n in (dp, tensor, tensor, dp):
        scratch += [dma((n - 1,)), dma((n - 1,))]
    dims = (dp, tensor, seq_rows, seq_len, vocab, all_seqs, tile)
    token_loss, coeff = pl.pallas_call(
        functools.partial(kernel, dims),
        out_shape=(
            jax.ShapeDtypeStruct((seq_rows, seq_len), F32),
            jax.ShapeDtypeStruct((wide, LANES), F32),
        ),
        in_specs=[pl.BlockSpec(memory_space=pl.ANY)] * len(args),
        out_specs=(pl.BlockSpec(memory_space=pltpu.VMEM), pl.BlockSpec(memory_space=pltpu.VMEM)),
        scratch_shapes=scratch,
        compiler_params=pltpu.CompilerParams(collective_id=0, has_side_effects=True),
        name="ppo",
    )(*args)
    grad = (coeff[:, 0:1] * value_weight.astype(F32)[None, :]).astype(BF16)
    return token_loss, grad.reshape(all_seqs, tile, feats)


def solution(mesh):
    in_specs = (
        P("dp", None, "tensor"),
        P("dp", None),
        P("dp", None),
        P("dp"),
        P("dp"),
        P("dp", None),
        P(None, "dp"),
        P("dp", None),
        P("dp", None),
        P(None, "dp", "tensor"),
        P("tensor"),
    )
    out_specs = (P("dp", None), P(None, "dp", "tensor"))
    return jax.shard_map(
        per_device, mesh=mesh, in_specs=in_specs, out_specs=out_specs, check_vma=False
    )
```

time: 71.9 us -> 21 us (0.29)
  blocking collectives: 30 us -> 0 us
  starting transfers between devices: 16 us -> 0 us
  Pallas kernels: 0 us -> 14.8 us
  waiting for transfers between devices: 12.2 us -> 0 us
  other arithmetic: 6.42 us -> 1.68 us
  matrix products: 2.1 us -> 0 us
    psum x2 -> x0, blocking collectives: 23.4 us -> none  [the longest x1 17.7 us: per_device(): lax.psum((moments[0], moments[1], moments[2]), 'dp')]
    all_to_all x3 -> x0, starting transfers between devices: 16 us -> none  [the longest x1 7.28 us: per_device(): lax.all_to_all(ref_logprob.astype(jnp.float32), 'dp', split_axis=0, conca...]
    pallas_call x0 -> x1, Pallas kernels: none -> 14.8 us  [per_device(): pl.pallas_call(functools.partial(kernel, dims), out_shape=(jax.ShapeDtype...]
    all_to_all x3 -> x0, waiting for transfers between devices: 12.2 us -> none  [the longest x1 6.41 us: per_device(): lax.all_to_all(local_part, 'dp', split_axis=0, concat_axis=1, tiled=True)]
    pmax x1 -> x0, blocking collectives: 6.63 us -> none  [per_device(): row_max = lax.pmax(local_top, 'tensor')]
    gather x1 -> x0, local copies, waits for them, and re-layouts: 2.81 us -> none  [per_device(): jnp.take_along_axis(logits, clipped_ids[:, :, None], axis=2)[:, :, 0]]
    reduce_max x1 -> x0, other arithmetic: 2.13 us -> none  [per_device(): local_top = jnp.max(logits, axis=2).astype(jnp.float32)]
    dot_general x4 -> x0, matrix products: 2.1 us -> none  [the longest x1 1.47 us: per_device(): jnp.dot(tile_rows, value_weight, preferred_element_type=jnp.float32)]
  transfers between devices with their start and end apart: 3 -> 0, of which waited for: 2 -> 0; matrix products, arithmetic and copies ran while one was open for 11% -> 0% of each run, Pallas kernels for 0% -> 0%
where the time goes in v1:
time: 21 us; the launch traced here: 20.7 us
  Pallas kernels  14.8 us (70%)
  local copies, waits for them, and re-layouts  3.59 us (17%)
  other arithmetic  1.68 us (8%)
  between operations  0.64 us (3%)
    pallas_call x1, Pallas kernels, per_device(): pl.pallas_call(functools.partial(kernel, dims), out_shape=(jax.ShapeDtype...  14.8 us
    convert_element_type x2, other arithmetic, per_device(): grad = (coeff[:, 0:1] * value_weight.astype(F32)[None, :]).astype(BF16)  1.68 us
    reshape x1, local copies, waits for them, and re-layouts, per_device(): value_weight.reshape(1, feats)  1.29 us
    unnamed x1, local copies, waits for them, and re-layouts  1.22 us
    slice x1, local copies, waits for them, and re-layouts, per_device(): grad = (coeff[:, 0:1] * value_weight.astype(F32)[None, :]).astype(BF16)  1.01 us

profile of v1, /device:TPU:0, one launch (start us, length us, event | category | flops | bytes accessed | tf_op | source)
XLA Modules:
  0.0 20.7 jit_solution(15441299679760434654)
XLA Ops:
  0.6 1.3 %reshape.23.weight_hbm = bf16[1,1280]{1,0:T(2,128)(2,1)} reshape(bf16[1280]{0:T(1024)(128)(2,1)} %param.21) | data formatting | bytes 5120 | tf_op jit(solution)/shard_map/reshape | solution.py:280
  1.9 0.7 %convert_element_type.7 = f32[1280]{0:T(1024)S(1)} convert(bf16[1280]{0:T(1024)(128)(2,1)} %param.21) | non-fusion elementwise | flops 1280 | bytes 7680 | tf_op jit(solution)/shard_map/convert_element_type | solution.py:305
  2.6 14.8 %ppo.1 = (f32[2,128]{1,0:T(2,128)}, f32[256,128]{1,0:T(8,128)}) custom-call(bf16[2,128,4864]{2,1,0:T(8,128)(2,1)} %logits_hbm.1, s32[2,128]{1,0:T(2,128)} %ids_hbm.1, s32[2,128]{1,0:T(2,128)} %mask_hbm.1, s32[2]{0:T(128)} %len_hbm.1, s32[2]{0:T(128)} %prompt_hbm.1, f32[2,128]{1,0:T(2,128)} %old_hbm.1, bf16[16,16]{1,0:T(8,128)(2,1)} %ref_hbm.1, ...), custom_call_target="tpu_custom_call" | custom-call | tf_op jit(solution)/shard_map/ppo/pallas_call | solution.py:293
  17.4 1.0 %slice_reduce_fusion = f32[256]{0:T(256)S(1)} fusion(f32[256,128]{1,0:T(8,128)} %get-tuple-element.5), kind=kLoop, calls=%fused_computation.1 | loop fusion | bytes 2048 | tf_op jit(solution)/shard_map/slice | solution.py:305
  18.4 0.1 mul.16
  18.5 1.0 %multiply_convert_fusion = bf16[16,16,1280]{2,1,0:T(8,128)(2,1)} fusion(f32[1280]{0:T(1024)S(1)} %convert_element_type.7, f32[16,16]{1,0:T(8,128)S(1)} %mul.16), kind=kLoop, calls=%fused_computation | loop fusion | flops 655360 | bytes 661504 | tf_op jit(solution)/shard_map/convert_element_type | solution.py:305
  19.5 1.2 %copy.14 = f32[2,128]{1,0:T(2,128)} copy(f32[2,128]{1,0:T(2,128)} %get-tuple-element.8) | data formatting | bytes 2048

commit v2 on v1

--- a/solution.py
+++ b/solution.py
@@ -12,6 +12,7 @@
 MESH = pl.DeviceIdType.MESH
 LANES = 128
 ROWS = 32
+PIECES = 4
 
 
 def select_dot(x, hot):
@@ -28,7 +29,7 @@
     dims,
     logits_hbm, ids_hbm, mask_hbm, len_hbm, prompt_hbm, old_hbm, ref_hbm, adv_hbm, ret_hbm,
     hidden_hbm, weight_hbm,
-    loss_ref, coeff_ref,
+    loss_ref, grad_ref,
     logits, ids, mask, lens, prompts, old, ref, adv, ret, hidden, weight,
     top_col, sum_col, hit_col, id_col,
     early, value_part, stats, value_sum,
@@ -93,11 +94,15 @@
 
     smalls[0].wait()
     smalls[1].wait()
-    head = jnp.broadcast_to(weight[...], (16, weight.shape[1]))
+    head_row = weight[...].reshape(1, weight.shape[0])
+    head = jnp.broadcast_to(head_row, (16, weight.shape[0]))
     part = lax.dot_general(
         head, hidden[...], (((1,), (1,)), ((), ())), preferred_element_type=F32
     )
     value_part[me_t] = part[:8]
+    pl.semaphore_wait(barrier, dp - 1 + tensor - 1)
+    for c in v_copies:
+        c.start()
 
     for c in smalls[2:]:
         c.wait()
@@ -132,6 +137,8 @@
         [ret_row, live, adv_row, prompt_row.astype(F32), ref_row, jnp.zeros((3, wide), F32)],
         axis=0,
     )
+    for c in e_copies:
+        c.start()
 
     start = me_t * vocab
     lane_block = lax.broadcasted_iota(jnp.int32, (ROWS, LANES), 1)
@@ -182,13 +189,6 @@
     split = (seq_rows + 1) // 2
     for r in range(split):
         logit_pass(r)
-    pl.semaphore_wait(barrier, dp - 1 + tensor - 1)
-    for c in v_copies + e_copies:
-        c.start()
-    for r in range(split, seq_rows):
-        logit_pass(r)
-    for c in s_copies:
-        c.start()
 
     for c in v_copies:
         c.wait_recv()
@@ -199,29 +199,42 @@
     for c in w_copies:
         c.start()
 
+    for r in range(split, seq_rows):
+        logit_pass(r)
+    for c in s_copies:
+        c.start()
+
     for c in e_copies:
         c.wait_recv()
-    rows_all = early[...].reshape(dp * 8, wide)
     k = lax.broadcasted_iota(jnp.int32, (wide, wide), 0)
     l = lax.broadcasted_iota(jnp.int32, (wide, wide), 1)
     to_tile = (k == ((l // tile) % seq_rows) * seq_len + me_dp * tile + l % tile).astype(F32)
     to_seq = (k == (me_dp * seq_rows + l // seq_len) * tile + l % tile).astype(F32)
     to_seq = to_seq.astype(BF16)
-    moved = select_dot(rows_all, to_tile.astype(BF16))
-    row_id = lax.broadcasted_iota(jnp.int32, (dp * 8, wide), 0)
-    lane_id = lax.broadcasted_iota(jnp.int32, (dp * 8, wide), 1)
-    from_seq = lane_id // (tile * seq_rows) * 8
+    row_id = lax.broadcasted_iota(jnp.int32, (dp, wide), 0)
+    lane_id = lax.broadcasted_iota(jnp.int32, (dp, wide), 1)
+    from_seq = row_id == lane_id // (tile * seq_rows)
+    from_tile = row_id == (lane_id % seq_len) // tile
 
     def fold(x, keep):
         return jnp.sum(jnp.where(keep, x, 0.0), axis=0, keepdims=True)
 
-    ret_tile = fold(moved, row_id == from_seq)
-    live_tile = fold(moved, row_id == from_seq + 1)
+    moved = select_dot(
+        jnp.concatenate([early[:, 0, :], early[:, 1, :]], axis=0), to_tile.astype(BF16)
+    )
+    ret_tile = fold(moved[:dp], from_seq)
+    live_tile = fold(moved[dp:], from_seq)
+    ref_seq = fold(
+        jnp.dot(early[:, 4, :].astype(BF16), to_seq, preferred_element_type=F32), from_tile
+    )
+
     coeff = 32.0 * live_tile * (value[0:1] - ret_tile)
+    head32 = head_row.astype(F32)
     for h in range(wide // LANES):
-        coeff_ref[h * LANES : (h + 1) * LANES, :] = column(coeff[:, h * LANES : (h + 1) * LANES])
-    from_tile = (lane_id % seq_len) // tile * 8
-    ref_seq = fold(select_dot(rows_all, to_seq), row_id == from_tile + 4)
+        factor = column(coeff[:, h * LANES : (h + 1) * LANES])
+        for c in range(head32.shape[1] // LANES):
+            cols = slice(c * LANES, (c + 1) * LANES)
+            grad_ref[h * LANES : (h + 1) * LANES, cols] = (factor * head32[:, cols]).astype(BF16)
 
     live_all = early[:, 1, :]
     adv_all = early[:, 2, :]
@@ -255,14 +268,27 @@
 
     for c in w_copies:
         c.wait_recv()
-    value_rows = value_sum[...].reshape(dp * 8, wide)
-    value_seq = fold(select_dot(value_rows, to_seq), row_id == from_tile)
+    value_seq = fold(select_dot(value_sum[:, 0, :], to_seq), from_tile)
     error = value_seq - ret_row
     loss = live * (policy + 0.25 * error * error)
     for r in range(seq_rows):
         loss_ref[r : r + 1, :] = loss[:, r * seq_len : (r + 1) * seq_len]
     for c in v_copies + e_copies + s_copies + w_copies:
         c.wait_send()
+
+
+def write_out(loss_in, grad_in, loss_ref, grad_ref, sems):
+    copies = [pltpu.make_async_copy(loss_in, loss_ref, sems.at[0])]
+    step = grad_in.shape[0] // PIECES
+    for n in range(PIECES):
+        rows = pl.ds(n * step, step)
+        copies.append(
+            pltpu.make_async_copy(grad_in.at[rows], grad_ref.at[rows], sems.at[n + 1])
+        )
+    for c in copies:
+        c.start()
+    for c in copies:
+        c.wait()
 
 
 def per_device(
@@ -277,10 +303,11 @@
     ref = ref_logprob if tile % 16 == 0 else ref_logprob.reshape(1, wide)
     args = (
         logits, token_ids, response_mask, lengths, prompt_of, old_logprob, ref, advantages,
-        returns, critic_hidden.reshape(all_seqs * tile, feats), value_weight.reshape(1, feats),
-    )
+        returns, critic_hidden.reshape(all_seqs * tile, feats), value_weight,
+    )
+    args = tuple(pltpu.with_memory_space_constraint(x, pltpu.HBM) for x in args)
     scratch = [
-        pltpu.SMEM(x.shape, x.dtype) if x.ndim == 1 else pltpu.VMEM(x.shape, x.dtype)
+        pltpu.SMEM(x.shape, x.dtype) if x.shape == (seq_rows,) else pltpu.VMEM(x.shape, x.dtype)
         for x in args
     ]
     scratch += [pltpu.VMEM((seq_len, LANES), t) for t in (F32, F32, F32, jnp.int32)]
@@ -290,19 +317,32 @@
     for n in (dp, tensor, tensor, dp):
         scratch += [dma((n - 1,)), dma((n - 1,))]
     dims = (dp, tensor, seq_rows, seq_len, vocab, all_seqs, tile)
-    token_loss, coeff = pl.pallas_call(
+    token_loss, grad = pl.pallas_call(
         functools.partial(kernel, dims),
         out_shape=(
             jax.ShapeDtypeStruct((seq_rows, seq_len), F32),
-            jax.ShapeDtypeStruct((wide, LANES), F32),
+            jax.ShapeDtypeStruct((wide, feats), BF16),
         ),
-        in_specs=[pl.BlockSpec(memory_space=pl.ANY)] * len(args),
+        in_specs=[pl.BlockSpec(memory_space=pltpu.HBM)] * len(args),
         out_specs=(pl.BlockSpec(memory_space=pltpu.VMEM), pl.BlockSpec(memory_space=pltpu.VMEM)),
         scratch_shapes=scratch,
-        compiler_params=pltpu.CompilerParams(collective_id=0, has_side_effects=True),
+        compiler_params=pltpu.CompilerParams(
+            collective_id=0, has_side_effects=True, vmem_limit_bytes=16 << 20
+        ),
         name="ppo",
     )(*args)
-    grad = (coeff[:, 0:1] * value_weight.astype(F32)[None, :]).astype(BF16)
+    token_loss, grad = pl.pallas_call(
+        write_out,
+        out_shape=(
+            jax.ShapeDtypeStruct((seq_rows, seq_len), F32),
+            jax.ShapeDtypeStruct((wide, feats), BF16),
+        ),
+        in_specs=[pl.BlockSpec(memory_space=pltpu.VMEM)] * 2,
+        out_specs=(pl.BlockSpec(memory_space=pltpu.HBM),) * 2,
+        scratch_shapes=[dma((PIECES + 1,))],
+        compiler_params=pltpu.CompilerParams(vmem_limit_bytes=16 << 20),
+        name="tail",
+    )(token_loss, grad)
     return token_loss, grad.reshape(all_seqs, tile, feats)
 
 

time: 21 us -> 14.7 us (0.70)
  local copies, waits for them, and re-layouts: 3.59 us -> 0 us
  other arithmetic: 1.68 us -> 0 us
  Pallas kernels: 14.8 us -> 13.9 us
    pallas_call x1, Pallas kernels: 14.8 us -> 13 us  [per_device(): pl.pallas_call(functools.partial(kernel, dims), out_shape=(jax.ShapeDtype...]
    convert_element_type x2 -> x0, other arithmetic: 1.68 us -> none  [per_device(): grad = (coeff[:, 0:1] * value_weight.astype(F32)[None, :]).astype(BF16)]
    reshape x1 -> x0, local copies, waits for them, and re-layouts: 1.29 us -> none  [per_device(): value_weight.reshape(1, feats)]
    unnamed x1 -> x0, local copies, waits for them, and re-layouts: 1.22 us -> none
    slice x1 -> x0, local copies, waits for them, and re-layouts: 1.01 us -> none  [per_device(): grad = (coeff[:, 0:1] * value_weight.astype(F32)[None, :]).astype(BF16)]
    pallas_call x0 -> x1, Pallas kernels: none -> 0.88 us  [per_device(): pl.pallas_call(write_out, out_shape=(jax.ShapeDtypeStruct((seq_rows, seq_...]
where the time goes in v2:
time: 14.7 us; the launch traced here: 14.6 us
  Pallas kernels  13.9 us (95%)
  between operations  0.64 us (4%)
    pallas_call x1, Pallas kernels, per_device(): pl.pallas_call(functools.partial(kernel, dims), out_shape=(jax.ShapeDtype...  13 us
    pallas_call x1, Pallas kernels, per_device(): pl.pallas_call(write_out, out_shape=(jax.ShapeDtypeStruct((seq_rows, seq_...  0.88 us

profile of v2, /device:TPU:0, one launch (start us, length us, event | category | flops | bytes accessed | tf_op | source)
XLA Modules:
  0.0 14.6 jit_solution(7011896350759875911)
XLA Ops:
  0.6 13.0 %ppo.1 = (f32[2,128]{1,0:T(2,128)S(1)}, bf16[256,1280]{1,0:T(8,128)(2,1)S(1)}) custom-call(bf16[2,128,4864]{2,1,0:T(8,128)(2,1)} %logits_hbm.1, s32[2,128]{1,0:T(2,128)} %ids_hbm.1, s32[2,128]{1,0:T(2,128)} %mask_hbm.1, s32[2]{0:T(128)} %len_hbm.1, s32[2]{0:T(128)} %prompt_hbm.1, f32[2,128]{1,0:T(2,128)} %old_hbm.1, bf16[16,16]{1,0:T(8,128)(2,1)} %ref_hbm.1, ...), custom_call_target="tpu_custom_call" | custom-call | tf_op jit(solution)/shard_map/ppo/pallas_call | solution.py:320
  13.7 0.9 %tail.1 = (f32[2,128]{1,0:T(2,128)}, bf16[256,1280]{1,0:T(8,128)(2,1)}) custom-call(f32[2,128]{1,0:T(2,128)S(1)} %get-tuple-element.6.loss_in, bf16[256,1280]{1,0:T(8,128)(2,1)S(1)} %get-tuple-element.7.grad_in), custom_call_target="tpu_custom_call" | custom-call | tf_op jit(solution)/shard_map/tail/pallas_call | solution.py:334

commit v3 on v2

--- a/solution.py
+++ b/solution.py
@@ -99,10 +99,7 @@
     part = lax.dot_general(
         head, hidden[...], (((1,), (1,)), ((), ())), preferred_element_type=F32
     )
-    value_part[me_t] = part[:8]
-    pl.semaphore_wait(barrier, dp - 1 + tensor - 1)
-    for c in v_copies:
-        c.start()
+    value_part[me_t] = part[:1]
 
     for c in smalls[2:]:
         c.wait()
@@ -133,12 +130,8 @@
         ref_row = jnp.sum(jnp.where(owner, ref_wide, 0.0), axis=0, keepdims=True)
     else:
         ref_row = ref[...].astype(F32)
-    early[me_dp] = jnp.concatenate(
-        [ret_row, live, adv_row, prompt_row.astype(F32), ref_row, jnp.zeros((3, wide), F32)],
-        axis=0,
-    )
-    for c in e_copies:
-        c.start()
+    code = live * (prompt_row.astype(F32) + 1.0)
+    early[me_dp] = jnp.concatenate([ret_row, code, adv_row, ref_row], axis=0)
 
     start = me_t * vocab
     lane_block = lax.broadcasted_iota(jnp.int32, (ROWS, LANES), 1)
@@ -185,10 +178,17 @@
             stats[me_t, 1:2, cols] = jnp.sum(sum_col[rows, :].T, axis=0, keepdims=True)
             stats[me_t, 2:3, cols] = jnp.sum(hit_col[rows, :].T, axis=0, keepdims=True)
 
-    stats[me_t, 3:8, :] = jnp.zeros((5, wide), F32)
+    stats[me_t, 3:4, :] = jnp.zeros((1, wide), F32)
     split = (seq_rows + 1) // 2
     for r in range(split):
         logit_pass(r)
+    pl.semaphore_wait(barrier, dp - 1 + tensor - 1)
+    for c in v_copies + e_copies:
+        c.start()
+    for r in range(split, seq_rows):
+        logit_pass(r)
+    for c in s_copies:
+        c.start()
 
     for c in v_copies:
         c.wait_recv()
@@ -197,11 +197,6 @@
         value = value + value_part[j]
     value_sum[me_dp] = value
     for c in w_copies:
-        c.start()
-
-    for r in range(split, seq_rows):
-        logit_pass(r)
-    for c in s_copies:
         c.start()
 
     for c in e_copies:
@@ -219,16 +214,18 @@
     def fold(x, keep):
         return jnp.sum(jnp.where(keep, x, 0.0), axis=0, keepdims=True)
 
+    code_all = early[:, 1, :]
+    live_all = jnp.where(code_all > 0.0, 1.0, 0.0)
     moved = select_dot(
-        jnp.concatenate([early[:, 0, :], early[:, 1, :]], axis=0), to_tile.astype(BF16)
+        jnp.concatenate([early[:, 0, :], live_all], axis=0), to_tile.astype(BF16)
     )
     ret_tile = fold(moved[:dp], from_seq)
     live_tile = fold(moved[dp:], from_seq)
     ref_seq = fold(
-        jnp.dot(early[:, 4, :].astype(BF16), to_seq, preferred_element_type=F32), from_tile
-    )
-
-    coeff = 32.0 * live_tile * (value[0:1] - ret_tile)
+        jnp.dot(early[:, 3, :].astype(BF16), to_seq, preferred_element_type=F32), from_tile
+    )
+
+    coeff = 32.0 * live_tile * (value - ret_tile)
     head32 = head_row.astype(F32)
     for h in range(wide // LANES):
         factor = column(coeff[:, h * LANES : (h + 1) * LANES])
@@ -236,12 +233,10 @@
             cols = slice(c * LANES, (c + 1) * LANES)
             grad_ref[h * LANES : (h + 1) * LANES, cols] = (factor * head32[:, cols]).astype(BF16)
 
-    live_all = early[:, 1, :]
     adv_all = early[:, 2, :]
-    prompt_all = early[:, 3, :]
     whitened = jnp.zeros((1, wide), F32)
     for r in range(seq_rows):
-        same = jnp.where(prompt_all == prompts[r].astype(F32), live_all, 0.0)
+        same = jnp.where(code_all == prompts[r].astype(F32) + 1.0, 1.0, 0.0)
         count = jnp.maximum(jnp.sum(same, keepdims=True), 1.0)
         mean = jnp.sum(same * adv_all, keepdims=True) / count
         off = adv_all - mean
@@ -311,7 +306,9 @@
         for x in args
     ]
     scratch += [pltpu.VMEM((seq_len, LANES), t) for t in (F32, F32, F32, jnp.int32)]
-    scratch += [pltpu.VMEM((n, 8, wide), F32) for n in (dp, tensor, tensor, dp)]
+    scratch += [
+        pltpu.VMEM((n, k, wide), F32) for n, k in ((dp, 4), (tensor, 1), (tensor, 4), (dp, 1))
+    ]
     dma = pltpu.SemaphoreType.DMA
     scratch += [dma((10,)), dma((seq_rows,))]
     for n in (dp, tensor, tensor, dp):

time: 14.7 us -> 15.7 us (1.068)
  Pallas kernels: 13.9 us -> 14.9 us
    pallas_call x1, Pallas kernels: 13 us -> 14 us  [per_device(): pl.pallas_call(functools.partial(kernel, dims), out_shape=(jax.ShapeDtype...]
where the time goes in v3:
time: 15.7 us; the launch traced here: 15.6 us
  Pallas kernels  14.9 us (95%)
  between operations  0.64 us (4%)
    pallas_call x1, Pallas kernels, per_device(): pl.pallas_call(functools.partial(kernel, dims), out_shape=(jax.ShapeDtype...  14 us
    pallas_call x1, Pallas kernels, per_device(): pl.pallas_call(write_out, out_shape=(jax.ShapeDtypeStruct((seq_rows, seq_...  0.88 us

profile of v3, /device:TPU:0, one launch (start us, length us, event | category | flops | bytes accessed | tf_op | source)
XLA Modules:
  0.0 15.6 jit_solution(6868534625290080637)
XLA Ops:
  0.6 14.0 %ppo.1 = (f32[2,128]{1,0:T(2,128)S(1)}, bf16[256,1280]{1,0:T(8,128)(2,1)S(1)}) custom-call(bf16[2,128,4864]{2,1,0:T(8,128)(2,1)} %logits_hbm.1, s32[2,128]{1,0:T(2,128)} %ids_hbm.1, s32[2,128]{1,0:T(2,128)} %mask_hbm.1, s32[2]{0:T(128)} %len_hbm.1, s32[2]{0:T(128)} %prompt_hbm.1, f32[2,128]{1,0:T(2,128)} %old_hbm.1, bf16[16,16]{1,0:T(8,128)(2,1)} %ref_hbm.1, ...), custom_call_target="tpu_custom_call" | custom-call | tf_op jit(solution)/shard_map/ppo/pallas_call | solution.py:317
  14.7 0.9 %tail.1 = (f32[2,128]{1,0:T(2,128)}, bf16[256,1280]{1,0:T(8,128)(2,1)}) custom-call(f32[2,128]{1,0:T(2,128)S(1)} %get-tuple-element.6.loss_in, bf16[256,1280]{1,0:T(8,128)(2,1)S(1)} %get-tuple-element.7.grad_in), custom_call_target="tpu_custom_call" | custom-call | tf_op jit(solution)/shard_map/tail/pallas_call | solution.py:331

commit v4 on v3

--- a/solution.py
+++ b/solution.py
@@ -55,6 +55,8 @@
         pltpu.make_async_copy(logits_hbm.at[r], logits.at[r], logit_sem.at[r])
         for r in range(seq_rows)
     ]
+    for c in smalls[:2]:
+        c.start()
     barrier = pltpu.get_barrier_semaphore()
     for d in range(1, dp):
         pl.semaphore_signal(
@@ -64,7 +66,7 @@
         pl.semaphore_signal(
             barrier, inc=1, device_id=(me_dp, lax.rem(me_t + d, tensor)), device_id_type=MESH
         )
-    for c in smalls + bigs:
+    for c in smalls[2:] + bigs:
         c.start()
 
     def over_dp(buf, send, recv):
@@ -100,6 +102,9 @@
         head, hidden[...], (((1,), (1,)), ((), ())), preferred_element_type=F32
     )
     value_part[me_t] = part[:1]
+    pl.semaphore_wait(barrier, dp - 1 + tensor - 1)
+    for c in v_copies:
+        c.start()
 
     for c in smalls[2:]:
         c.wait()
@@ -132,6 +137,8 @@
         ref_row = ref[...].astype(F32)
     code = live * (prompt_row.astype(F32) + 1.0)
     early[me_dp] = jnp.concatenate([ret_row, code, adv_row, ref_row], axis=0)
+    for c in e_copies:
+        c.start()
 
     start = me_t * vocab
     lane_block = lax.broadcasted_iota(jnp.int32, (ROWS, LANES), 1)
@@ -179,13 +186,7 @@
             stats[me_t, 2:3, cols] = jnp.sum(hit_col[rows, :].T, axis=0, keepdims=True)
 
     stats[me_t, 3:4, :] = jnp.zeros((1, wide), F32)
-    split = (seq_rows + 1) // 2
-    for r in range(split):
-        logit_pass(r)
-    pl.semaphore_wait(barrier, dp - 1 + tensor - 1)
-    for c in v_copies + e_copies:
-        c.start()
-    for r in range(split, seq_rows):
+    for r in range(seq_rows):
         logit_pass(r)
     for c in s_copies:
         c.start()

time: 15.7 us -> 14.4 us (0.917)
  Pallas kernels: 14.9 us -> 13.6 us
    pallas_call x1, Pallas kernels: 14 us -> 12.7 us  [per_device(): pl.pallas_call(functools.partial(kernel, dims), out_shape=(jax.ShapeDtype...]
where the time goes in v4:
time: 14.4 us; the launch traced here: 14.3 us
  Pallas kernels  13.6 us (94%)
  between operations  0.64 us (4%)
    pallas_call x1, Pallas kernels, per_device(): pl.pallas_call(functools.partial(kernel, dims), out_shape=(jax.ShapeDtype...  12.7 us
    pallas_call x1, Pallas kernels, per_device(): pl.pallas_call(write_out, out_shape=(jax.ShapeDtypeStruct((seq_rows, seq_...  0.88 us

profile of v4, /device:TPU:0, one launch (start us, length us, event | category | flops | bytes accessed | tf_op | source)
XLA Modules:
  0.0 14.3 jit_solution(1893553076520514365)
XLA Ops:
  0.6 12.7 %ppo.1 = (f32[2,128]{1,0:T(2,128)S(1)}, bf16[256,1280]{1,0:T(8,128)(2,1)S(1)}) custom-call(bf16[2,128,4864]{2,1,0:T(8,128)(2,1)} %logits_hbm.1, s32[2,128]{1,0:T(2,128)} %ids_hbm.1, s32[2,128]{1,0:T(2,128)} %mask_hbm.1, s32[2]{0:T(128)} %len_hbm.1, s32[2]{0:T(128)} %prompt_hbm.1, f32[2,128]{1,0:T(2,128)} %old_hbm.1, bf16[16,16]{1,0:T(8,128)(2,1)} %ref_hbm.1, ...), custom_call_target="tpu_custom_call" | custom-call | tf_op jit(solution)/shard_map/ppo/pallas_call | solution.py:318
  13.4 0.9 %tail.1 = (f32[2,128]{1,0:T(2,128)}, bf16[256,1280]{1,0:T(8,128)(2,1)}) custom-call(f32[2,128]{1,0:T(2,128)S(1)} %get-tuple-element.6.loss_in, bf16[256,1280]{1,0:T(8,128)(2,1)S(1)} %get-tuple-element.7.grad_in), custom_call_target="tpu_custom_call" | custom-call | tf_op jit(solution)/shard_map/tail/pallas_call | solution.py:332
